TPU v7x, 32 devices: a whole 2x2x4 slice. The times are simulated.
32 devices in a mesh: gx: 8 (over y, x, core), gy: 4 (over z).
Axes of the slice: x: 2, y: 2, z: 4, core: 2. Of those that a mesh axis runs over, the one named last changes fastest.
Arguments:
- right_side: float32 [32, 256, 256], P('gx', 'gy'), may hold values from -40 to 40
- kappa_sq: float32 [32, 256, 256], P('gx', 'gy'), may hold values from 0.5 to 4
Outputs:
- solution_field: float32 [32, 256, 256], P('gx', 'gy')
- residual: float32 [32, 256, 256], P('gx', 'gy')
- residual_rms: float32 [3], replicated
All inputs are finite; a program needn't handle non-finite values.
Results may differ from a plain program's by a relative error of at most 0.00016.
Values sent between devices are 32-bit elements; how exact they have to be, the bound alone decides.
A program may use at most 64 MiB of HBM per device.

v0:
```python
import functools
import jax
import jax.numpy as jnp
from jax import lax
from jax.experimental import pallas as pl
from jax.experimental.pallas import tpu as pltpu
from jax.sharding import PartitionSpec as P

ITERS = 3
MESH = pl.DeviceIdType.MESH


def shifted(c):
    return [None] + c[:-1]


def plus(a, b, scale):
    out = []
    for one, two in zip(a, b):
        two = None if two is None else two * scale
        out.append(one if two is None else two if one is None else one + two)
    return out


def form(c, entry):
    total = None
    for i, one in enumerate(c):
        for j, two in enumerate(c):
            if one is not None and two is not None and i < ITERS and j < ITERS:
                term = one * two * entry(i, j)
                total = term if total is None else total + term
    return total


def coefficients(mu, dots, cells):
    one = jnp.ones_like(mu[0])
    res = [one] + [None] * ITERS
    step = [None] * (ITERS + 1)
    sol = [None] * (ITERS + 1)
    norms = []
    for i in range(ITERS):
        gamma = form(res, lambda a, b: mu[a + b])
        delta = form(res, lambda a, b: mu[a + b + 1])
        norms.append(jnp.sqrt(form(res, lambda a, b: dots[min(a, b), max(a, b)]) / cells))
        if i == 0:
            alpha = gamma / delta
            step = list(res)
        else:
            beta = gamma / gamma_old
            alpha = gamma / (delta - beta * gamma / alpha_old)
            step = plus(res, step, beta)
        sol = plus(sol, step, alpha)
        res = plus(res, shifted(step), -alpha)
        gamma_old, alpha_old = gamma, alpha
    return sol, res, norms


def kernel(
    nx, ny, cells, rhs_hbm, kappa_hbm, *refs,
):
    (
    v_ref, y_ref, coef_ref, t_ref, d_ref, m_ref, face_ref, edge_out, edge_in, corner_out, corner_in,
    slots, load_sem, face_send, face_recv, edge_send, edge_recv, corner_send, corner_recv,
    sum_send, sum_recv,
    ) = refs
    layers, rows, cols = rhs_hbm.shape
    ix, iy = lax.axis_index("gx"), lax.axis_index("gy")
    count = nx * ny
    me = ix * ny + iy
    load_k = pltpu.make_async_copy(kappa_hbm, d_ref, load_sem.at[0])
    load_r = pltpu.make_async_copy(rhs_hbm, v_ref.at[0], load_sem.at[1])
    load_k.start()
    load_r.start()

    barrier = pltpu.get_barrier_semaphore()

    near = ny // 2 <= ITERS

    def greet(x, y):
        pl.semaphore_signal(barrier, inc=1, device_id=(x, y), device_id_type=MESH)

    def greet_any(k, carry):
        other = lax.rem(me + k, count)
        greet(other // ny, lax.rem(other, ny))
        return carry

    def greet_x(k, carry):
        greet(lax.rem(ix + k, nx), iy)
        return carry

    def greet_y(k, carry):
        greet(ix, lax.rem(iy + k, ny))
        return carry

    if near:
        lax.fori_loop(1, ny, greet_y, 0)
        lax.fori_loop(1, nx, greet_x, 0)
        greetings = nx - 1 + ny - 1
    else:
        lax.fori_loop(1, count, greet_any, 0)
        greetings = count - 1

    x_of = (lax.rem(ix + nx - 1, nx), lax.rem(ix + 1, nx))
    y_of = (lax.rem(iy + ny - 1, ny), lax.rem(iy + 1, ny))
    row = lax.broadcasted_iota(jnp.int32, (rows, cols), 0)
    first, last = row == 0, row == rows - 1

    def lateral(x):
        up = jnp.where(first, 0.0, pltpu.roll(x, 1, 0))
        down = jnp.where(last, 0.0, pltpu.roll(x, rows - 1, 0))
        return (pltpu.roll(x, 1, 1) + pltpu.roll(x, cols - 1, 1)) + (up + down)

    def local_k(get, l):
        x = get(l)
        out = d_ref[l] * x - lateral(x)
        if l > 0:
            out = out - get(l - 1)
        if l < layers - 1:
            out = out - get(l + 1)
        return out

    def tile_sum(x):
        return jnp.sum(x, axis=(0, 1), keepdims=True)

    load_k.wait()
    for l in range(layers):
        d = 6.0 + d_ref[l]
        d_ref[l] = d
        m_ref[l] = 1.0 / (d * d + 6.0)
    load_r.wait()

    ends = (0, layers - 1)
    mu, dots = ([], {})
    sends = []
    order = [0, layers - 1] + list(range(1, layers - 1)) if layers > 1 else [0]
    inner_first = list(range(1, layers - 1)) + [0, layers - 1] if layers > 1 else [0]

    def remote(src, dst, send, recv, device):
        copy = pltpu.make_async_remote_copy(
            src_ref=src, dst_ref=dst, send_sem=send, recv_sem=recv,
            device_id=device, device_id_type=MESH,
        )
        sends.append(copy)
        return copy

    for j in range(ITERS):
        for l in order:
            y_ref[j, l] = m_ref[l] * v_ref[j, l]
        for side in range(2):
            at = pl.ds((0, rows - 1)[side], 1)
            for k in range(2):
                corner_out[j, 2 * k + side] = y_ref[j, ends[k], at, :]
            for l in range(layers):
                edge_out[j, 0, side, l] = y_ref[j, l, at, :]
        if j == 0:
            pl.semaphore_wait(barrier, greetings)
        edges = [
            [
                remote(
                    edge_out.at[j, part, side], edge_in.at[j, part, 1 - side],
                    edge_send.at[j, part, side], edge_recv.at[j, part, 1 - side],
                    (ix, y_of[side]),
                )
                for side in range(2)
            ]
            for part in range(2)
        ]
        relayed = near and j == 0
        corners = [
            remote(
                edge_in.at[j, 0, side, ends[k]] if relayed else corner_out.at[j, 2 * k + side],
                corner_in.at[j, 2 * (1 - k) + (side if relayed else 1 - side)],
                corner_send.at[j, 2 * k + side],
                corner_recv.at[j, 2 * (1 - k) + (side if relayed else 1 - side)],
                (x_of[k], iy if relayed else y_of[side]),
            )
            for k in range(2)
            for side in range(2)
        ]
        faces = [
            [
                remote(
                    src.at[j, ends[k]], face_ref.at[j, 1 - k, part],
                    face_send.at[j, k, part], face_recv.at[j, 1 - k, part],
                    (x_of[k], iy),
                )
                for k in range(2)
            ]
            for part, src in enumerate((y_ref, t_ref))
        ]
        for copy in edges[0] + ([] if relayed else corners) + faces[0]:
            copy.start()
        get_y = lambda l: y_ref[j, l]
        for l in order:
            t_ref[j, l] = local_k(get_y, l)
        for side in range(2):
            for l in range(layers):
                at = pl.ds((0, rows - 1)[side], 1)
                edge_out[j, 1, side, l] = t_ref[j, l, at, :]
        for copy in edges[1] + faces[1]:
            copy.start()
        mu.append(tile_sum(sum(v_ref[j, l] * y_ref[j, l] for l in range(layers))))
        for i in range(j + 1):
            dots[i, j] = tile_sum(sum(v_ref[i, l] * v_ref[j, l] for l in range(layers)))
        for side in range(2):
            edges[0][1 - side].wait_recv()
            if relayed:
                corners[side].start()
                corners[2 + side].start()
        for copy in faces[0]:
            copy.wait_recv()
        full = ITERS + j % 2
        for l in range(layers):
            t = t_ref[j, l]
            if l == 0:
                t = t - face_ref[j, 0, 0]
            if l == layers - 1:
                t = t - face_ref[j, 1, 0]
            t_ref[full, l] = t
            for side in range(2):
                at = pl.ds((0, rows - 1)[side], 1)
                t_ref[full, l, at, :] = t_ref[full, l, at, :] - edge_in[j, 0, side, l]
        mu.append(tile_sum(sum(t_ref[full, l] * t_ref[full, l] for l in range(layers))))
        if j == ITERS - 1:
            start_sums(mu, dots, slots, sum_send, sum_recv, me, nx, ny)
        get_t = lambda l: t_ref[full, l]
        for l in range(layers):
            v = local_k(get_t, l)
            for k in range(2):
                if l == ends[k]:
                    v = v + y_ref[j, l]
            v_ref[j + 1, l] = v
            for side in range(2):
                at = pl.ds((0, rows - 1)[side], 1)
                v_ref[j + 1, l, at, :] = v_ref[j + 1, l, at, :] + y_ref[j, l, at, :]
        for copy in edges[1] + corners:
            copy.wait_recv()
        for l in range(layers):
            for side in range(2):
                at = pl.ds((0, rows - 1)[side], 1)
                line = v_ref[j + 1, l, at, :] - edge_in[j, 1, side, l]
                for k in range(2):
                    if l == ends[k]:
                        line = line + 2.0 * corner_in[j, 2 * k + side]
                v_ref[j + 1, l, at, :] = line
        for copy in faces[1]:
            copy.wait_recv()
        for k in range(2):
            v_ref[j + 1, ends[k]] = v_ref[j + 1, ends[k]] - face_ref[j, k, 1]

    for copy in sends:
        copy.wait_send()
    all_slots = slots.at[pl.ds(0, count - 1)]
    pltpu.make_async_copy(all_slots, all_slots, sum_send).wait()
    pltpu.make_async_copy(all_slots, all_slots, sum_recv).wait()
    total = jnp.sum(slots[...], axis=0)
    names = [("mu", i) for i in range(2 * ITERS)] + sorted(dots)
    got = {
        name: jnp.broadcast_to(total[:, k : k + 1], total.shape) for k, name in enumerate(names)
    }
    mu = [got["mu", i] for i in range(2 * ITERS)]
    sol, res, norms = coefficients(mu, got, float(cells))
    for k, value in enumerate(norms + sol[:ITERS] + res[1:]):
        coef_ref[k] = value[0, 0]


def start_sums(mu, dots, slots, sum_send, sum_recv, me, nx, ny):
    lane = lax.broadcasted_iota(jnp.int32, (1, slots.shape[-1]), 1)
    line = jnp.zeros(lane.shape, jnp.float32)
    for k, value in enumerate(mu + [dots[name] for name in sorted(dots)]):
        line = jnp.where(lane == k, value, line)
    slots[me] = line

    def send(x, y):
        pltpu.make_async_remote_copy(
            src_ref=slots.at[me],
            dst_ref=slots.at[me],
            send_sem=sum_send,
            recv_sem=sum_recv,
            device_id=(x, y),
            device_id_type=MESH,
        ).start()

    ix, iy = lax.axis_index("gx"), lax.axis_index("gy")
    y_at = [lax.rem(iy + k, ny) for k in range(ny)]

    def send_line(k, carry):
        x = ix + k
        x = jnp.where(x >= nx, x - nx, x)
        for y in y_at[1:] + y_at[:1]:
            send(x, y)
        return carry

    lax.fori_loop(1, nx, send_line, 0)
    for y in y_at[1:]:
        send(ix, y)


def finish(coef, v_ref, y_ref, sol_ref, res_ref, norms_ref):
    for i in range(ITERS):
        norms_ref[i] = coef[i]
    for l in range(v_ref.shape[1]):
        sol = coef[ITERS] * y_ref[0, l]
        res = v_ref[0, l]
        for i in range(1, ITERS):
            sol = sol + coef[ITERS + i] * y_ref[i, l]
        for i in range(1, ITERS + 1):
            res = res + coef[2 * ITERS + i - 1] * v_ref[i, l]
        sol_ref[l] = sol
        res_ref[l] = res


def body(right_side, kappa_sq):
    nx, ny = lax.axis_size("gx"), lax.axis_size("gy")
    shape = right_side.shape
    layers, rows, cols = shape
    cells = nx * layers * ny * rows * cols
    f32 = jnp.float32
    dma = pltpu.SemaphoreType.DMA
    whole = pl.BlockSpec(memory_space=pltpu.VMEM)
    smem = pl.BlockSpec(memory_space=pltpu.SMEM)
    out = pl.pallas_call(
        functools.partial(kernel, nx, ny, cells),
        out_shape=(
            pltpu.VMEM((ITERS + 1,) + shape, f32),
            pltpu.VMEM((ITERS,) + shape, f32),
            pltpu.SMEM((3 * ITERS,), f32),
        ),
        in_specs=[pl.BlockSpec(memory_space=pl.ANY)] * 2,
        out_specs=(whole, whole, smem),
        scratch_shapes=[
            pltpu.VMEM((ITERS + 2,) + shape, f32),
            pltpu.VMEM(shape, f32),
            pltpu.VMEM(shape, f32),
            pltpu.VMEM((ITERS, 2, 2, rows, cols), f32),
            pltpu.VMEM((ITERS, 2, 2, layers, 1, cols), f32),
            pltpu.VMEM((ITERS, 2, 2, layers, 1, cols), f32),
            pltpu.VMEM((ITERS, 4, 1, cols), f32),
            pltpu.VMEM((ITERS, 4, 1, cols), f32),
            pltpu.VMEM((nx * ny, 1, 128), f32),
            dma((2,)),
            dma((ITERS, 2, 2)),
            dma((ITERS, 2, 2)),
            dma((ITERS, 2, 2)),
            dma((ITERS, 2, 2)),
            dma((ITERS, 4)),
            dma((ITERS, 4)),
            dma(()),
            dma(()),
        ],
        compiler_params=pltpu.CompilerParams(collective_id=0, has_side_effects=True),
    )(right_side, kappa_sq)
    return pl.pallas_call(
        finish,
        out_shape=(
            jax.ShapeDtypeStruct(shape, f32),
            jax.ShapeDtypeStruct(shape, f32),
            jax.ShapeDtypeStruct((ITERS,), f32),
        ),
        in_specs=[smem, whole, whole],
        out_specs=(whole, whole, smem),
    )(out[2], *(pltpu.with_memory_space_constraint(x, pltpu.VMEM) for x in out[:2]))


def solution(mesh):
    return jax.shard_map(
        body,
        mesh=mesh,
        in_specs=(P("gx", "gy", None), P("gx", "gy", None)),
        out_specs=(P("gx", "gy", None), P("gx", "gy", None), P()),
        check_vma=False,
    )
```

profile of v0, /device:TPU:0, one launch (start us, length us, event | category | flops | bytes accessed | tf_op | source)
XLA Modules:
  0.0 26.5 jit_solution(8825708983955300367)
XLA Ops:
  0.6 25.0 %shard_map.49 = (f32[4,4,64,256]{3,2,1,0:T(8,128)S(1)}, f32[3,4,64,256]{3,2,1,0:T(8,128)S(1)}, f32[9]{0:T(128)S(4)}) custom-call(f32[4,64,256]{2,1,0:T(8,128)} %rhs_hbm.1, f32[4,64,256]{2,1,0:T(8,128)} %kappa_hbm.1), custom_call_target="tpu_custom_call" | custom-call | tf_op jit(solution)/shard_map/pallas_call | solution.py:322
  25.6 0.9 %shard_map.50 = (f32[4,64,256]{2,1,0:T(8,128)}, f32[4,64,256]{2,1,0:T(8,128)}, f32[3]{0:T(128)}) custom-call(f32[9]{0:T(128)S(4)} %get-tuple-element.6.coef, f32[4,4,64,256]{3,2,1,0:T(8,128)S(1)} %get-tuple-element.7.v_ref, f32[3,4,64,256]{3,2,1,0:T(8,128)S(1)} %get-tuple-element.8.y_ref), custom_call_target="tpu_custom_call" | custom-call | tf_op jit(solution)/shard_map/pallas_call | solution.py:353
where the time goes:
time: 26.7 us; the launch traced here: 26.5 us
  Pallas kernels  25.9 us (97%)
  between operations  0.64 us (2%)
    pallas_call x1, Pallas kernels, body(): pl.pallas_call(functools.partial(kernel, nx, ny, cells), out_shape=(pltpu...  25 us
    pallas_call x1, Pallas kernels, body(): pl.pallas_call(finish, out_shape=(jax.ShapeDtypeStruct(shape, f32), jax.S...  0.89 us

commit v1 on v0

v1 whole, which is shorter than its diff:
```python
import functools
import jax
import jax.numpy as jnp
from jax import lax
from jax.experimental import pallas as pl
from jax.experimental.pallas import tpu as pltpu
from jax.sharding import PartitionSpec as P

ITERS = 3
MESH = pl.DeviceIdType.MESH


def shifted(c):
    return [None] + c[:-1]


def plus(a, b, scale):
    out = []
    for one, two in zip(a, b):
        two = None if two is None else two * scale
        out.append(one if two is None else two if one is None else one + two)
    return out


def form(c, entry):
    total = None
    for i, one in enumerate(c):
        for j, two in enumerate(c):
            if one is not None and two is not None and i < ITERS and j < ITERS:
                term = one * two * entry(i, j)
                total = term if total is None else total + term
    return total


def coefficients(mu, dots, cells):
    one = jnp.ones_like(mu[0])
    res = [one] + [None] * ITERS
    step = [None] * (ITERS + 1)
    sol = [None] * (ITERS + 1)
    norms = []
    for i in range(ITERS):
        gamma = form(res, lambda a, b: mu[a + b])
        delta = form(res, lambda a, b: mu[a + b + 1])
        norms.append(jnp.sqrt(form(res, lambda a, b: dots[min(a, b), max(a, b)]) / cells))
        if i == 0:
            alpha = gamma / delta
            step = list(res)
        else:
            beta = gamma / gamma_old
            alpha = gamma / (delta - beta * gamma / alpha_old)
            step = plus(res, step, beta)
        sol = plus(sol, step, alpha)
        res = plus(res, shifted(step), -alpha)
        gamma_old, alpha_old = gamma, alpha
    return sol, res, norms


FACES = ("y0", "t0", "d", "y1", "t1", "w1", "t2")
SLOT = {name: i for i, name in enumerate(FACES)}
OUTER, INNER_ROW, INNER_LAYER, PARTIAL = 1, 2, 3, 4


def kernel(
    nx, ny, cells, rhs_hbm, kappa_hbm, *refs,
):
    (
    v_ref, y_ref, coef_ref, t_ref, f_ref, w_ref, d_ref, m_ref, pre_ref, face_ref, edge_out, edge_in,
    corner_out, corner_in, slots, load_sem, face_send, face_recv, edge_send, edge_recv,
    corner_send, corner_recv, sum_send, sum_recv,
    ) = refs
    layers, rows, cols = rhs_hbm.shape
    assert layers >= 3 and rows >= 3
    ix, iy = lax.axis_index("gx"), lax.axis_index("gy")
    count = nx * ny
    me = ix * ny + iy
    ends, seconds = (0, layers - 1), (1, layers - 2)
    order = [0, layers - 1] + list(range(1, layers - 1))
    inside = list(range(1, layers - 1))
    loads = {}
    for l in order:
        loads[l] = (
            pltpu.make_async_copy(kappa_hbm.at[l], d_ref.at[l], load_sem.at[0, l]),
            pltpu.make_async_copy(rhs_hbm.at[l], v_ref.at[0, l], load_sem.at[1, l]),
        )
        for copy in loads[l]:
            copy.start()

    barrier = pltpu.get_barrier_semaphore()
    x_of = (lax.rem(ix + nx - 1, nx), lax.rem(ix + 1, nx))
    y_of = (lax.rem(iy + ny - 1, ny), lax.rem(iy + 1, ny))

    near = ny // 2 <= 2

    def greet(x, y):
        pl.semaphore_signal(barrier, inc=1, device_id=(x, y), device_id_type=MESH)

    def greet_any(k, carry):
        other = lax.rem(me + k, count)
        greet(other // ny, lax.rem(other, ny))
        return carry

    def greet_x(k, carry):
        greet(lax.rem(ix + k, nx), iy)
        return carry

    def greet_y(k, carry):
        greet(ix, lax.rem(iy + k, ny))
        return carry

    if near:
        for x in x_of:
            for y in y_of:
                greet(x, y)
        lax.fori_loop(1, ny, greet_y, 0)
        lax.fori_loop(1, nx, greet_x, 0)
        greetings = nx - 1 + ny - 1 + 4
    else:
        lax.fori_loop(1, count, greet_any, 0)
        greetings = count - 1

    row = lax.broadcasted_iota(jnp.int32, (rows, cols), 0)
    first, last = row == 0, row == rows - 1

    def across(x):
        return pltpu.roll(x, 1, 1) + pltpu.roll(x, cols - 1, 1)

    def lateral(x):
        up = jnp.where(first, 0.0, pltpu.roll(x, 1, 0))
        down = jnp.where(last, 0.0, pltpu.roll(x, rows - 1, 0))
        return across(x) + (up + down)

    def local_k(get, l):
        x = get(l)
        out = d_ref[l] * x - lateral(x)
        if l > 0:
            out = out - get(l - 1)
        if l < layers - 1:
            out = out - get(l + 1)
        return out

    def tile_sum(x):
        return jnp.sum(x, axis=(0, 1), keepdims=True)

    def dot(a, b):
        return tile_sum(sum(a(l) * b(l) for l in range(layers)))

    at = [pl.ds((0, rows - 1)[side], 1) for side in range(2)]
    at_second = [pl.ds((1, rows - 2)[side], 1) for side in range(2)]
    sends = []

    def remote(src, dst, send, recv, device):
        copy = pltpu.make_async_remote_copy(
            src_ref=src, dst_ref=dst, send_sem=send, recv_sem=recv,
            device_id=device, device_id_type=MESH,
        )
        sends.append(copy)
        return copy

    def edges(name, src):
        n = SLOT[name]
        out = []
        for side in range(2):
            for l in range(layers):
                edge_out[n, side, l] = src[l, at[side], :]
        for side in range(2):
            copy = remote(
                edge_out.at[n, side], edge_in.at[n, 1 - side],
                edge_send.at[n, side], edge_recv.at[n, 1 - side], (ix, y_of[side]),
            )
            copy.start()
            out.append(copy)
        return out

    def faces(name, src):
        n = SLOT[name]
        out = []
        for k in range(2):
            copy = remote(
                src.at[ends[k]], face_ref.at[n, 1 - k],
                face_send.at[n, k], face_recv.at[n, 1 - k], (x_of[k], iy),
            )
            copy.start()
            out.append(copy)
        return out

    def corners(n, start, size):
        out = []
        for k in range(2):
            for side in range(2):
                q, there = 2 * k + side, 2 * (1 - k) + 1 - side
                copy = remote(
                    corner_out.at[q, pl.ds(start, size)], corner_in.at[there, pl.ds(start, size)],
                    corner_send.at[n, q], corner_recv.at[n, there], (x_of[k], y_of[side]),
                )
                copy.start()
                out.append(copy)
        return out

    def arrive(copies):
        for copy in copies:
            copy.wait_recv()

    def edge(name, side, l):
        return edge_in[SLOT[name], side, l]

    def face(name, k):
        return face_ref[SLOT[name], k]

    def corner(k, side, part):
        return corner_in[2 * k + side, part]

    mu, dots = ([], {})

    def full_t(j):
        for l in range(layers):
            t = t_ref[j, l]
            for k in range(2):
                if l == ends[k]:
                    t = t - face(f"y{j}", k)
            f_ref[l] = t
            for side in range(2):
                f_ref[l, at[side], :] = f_ref[l, at[side], :] - edge(f"y{j}", side, l)
        mu.append(dot(lambda l: f_ref[l], lambda l: f_ref[l]))

    def next_v(j):
        for l in order:
            v = local_k(lambda n: f_ref[n], l)
            if l in ends:
                v = v + y_ref[j, l]
            v_ref[j + 1, l] = v
            for side in range(2):
                v_ref[j + 1, l, at[side], :] = v_ref[j + 1, l, at[side], :] + y_ref[j, l, at[side], :]

    def next_rows(j, part):
        for l in order:
            for side in range(2):
                line = v_ref[j + 1, l, at[side], :] - edge(f"t{j}", side, l)
                for k in range(2):
                    if l == ends[k]:
                        line = line + 2.0 * corner(k, side, part)
                v_ref[j + 1, l, at[side], :] = line

    for l in order:
        for copy in loads[l]:
            copy.wait()
        d = 6.0 + d_ref[l]
        d_ref[l] = d
        m_ref[l] = 1.0 / (d * d + 6.0)
        y_ref[0, l] = m_ref[l] * v_ref[0, l]
    pl.semaphore_wait(barrier, greetings)
    y_edges = edges("y0", y_ref.at[0])
    for k in range(2):
        for side in range(2):
            corner_out[2 * k + side, 0] = y_ref[0, ends[k], at[side], :]
    y_corners = corners(0, 0, 1)
    y_faces = faces("y0", y_ref.at[0])
    for l in order:
        t_ref[0, l] = local_k(lambda n: y_ref[0, n], l)
    t_edges = edges("t0", t_ref.at[0])
    t_faces = faces("t0", t_ref.at[0])
    d_edges = edges("d", d_ref)
    d_faces = faces("d", d_ref)
    mu.append(dot(lambda l: v_ref[0, l], lambda l: y_ref[0, l]))
    dots[0, 0] = dot(lambda l: v_ref[0, l], lambda l: v_ref[0, l])
    arrive(y_edges + y_faces)
    full_t(0)
    next_v(0)
    arrive(t_edges + y_corners)
    next_rows(0, 0)
    for l in inside:
        y_ref[1, l] = m_ref[l] * v_ref[1, l]
    arrive(t_faces)
    for k in range(2):
        v = v_ref[1, ends[k]] - face("t0", k)
        v_ref[1, ends[k]] = v
        y_ref[1, ends[k]] = m_ref[ends[k]] * v
    y_edges = edges("y1", y_ref.at[1])
    for k in range(2):
        for side in range(2):
            q = 2 * k + side
            corner_out[q, OUTER] = y_ref[1, ends[k], at[side], :]
            corner_out[q, INNER_ROW] = y_ref[1, ends[k], at_second[side], :]
            corner_out[q, INNER_LAYER] = y_ref[1, seconds[k], at[side], :]
    y_corners = corners(1, OUTER, 3)
    y_faces = faces("y1", y_ref.at[1])
    for l in order:
        t_ref[1, l] = local_k(lambda n: y_ref[1, n], l)
    t_edges = edges("t1", t_ref.at[1])
    for k in range(2):
        for side in range(2):
            corner_out[2 * k + side, PARTIAL] = t_ref[1, ends[k], at[side], :]
    t_corners = corners(2, PARTIAL, 1)
    t_faces = faces("t1", t_ref.at[1])
    for l in order:
        w_ref[l] = local_k(lambda n: t_ref[1, n], l)
    w_edges = edges("w1", w_ref)
    w_faces = faces("w1", w_ref)
    mu.append(dot(lambda l: v_ref[1, l], lambda l: y_ref[1, l]))
    for i in range(2):
        dots[i, 1] = dot(lambda l: v_ref[i, l], lambda l: v_ref[1, l])
    arrive(y_edges + y_faces)
    full_t(1)
    next_v(1)
    arrive(t_edges + y_corners + t_corners + d_edges)
    next_rows(1, OUTER)
    for l in inside:
        y_ref[2, l] = m_ref[l] * v_ref[2, l]
    past = {
        (k, side): corner(k, side, PARTIAL) - (edge("y1", side, ends[k]) + face_ref[SLOT["y1"], k, at[side], :])
        for k in range(2)
        for side in range(2)
    }
    edge_part = {}
    for side in range(2):
        lines = []
        for l in range(layers):
            line = y_ref[1, l, at[side], :]
            for k in range(2):
                if l == ends[k]:
                    line = line + corner(k, side, OUTER)
            lines.append(line)
        for l in range(layers):
            beside = across(lines[l])
            if l > 0:
                beside = beside + lines[l - 1]
            if l < layers - 1:
                beside = beside + lines[l + 1]
            part = beside - edge("d", side, l) * lines[l] - f_ref[l, at[side], :]
            for k in range(2):
                if l == ends[k]:
                    part = part + (corner(k, side, INNER_ROW) - past[k, side])
            edge_part[side, l] = part
    arrive(d_faces)
    for k in range(2):
        pre_ref[k] = y_ref[1, ends[k]]
        for side in range(2):
            pre_ref[k, at[side], :] = pre_ref[k, at[side], :] + corner(k, side, OUTER)
        a = pre_ref[k]
        pre_ref[k] = lateral(a) - face("d", k) * a - f_ref[ends[k]]
        for side in range(2):
            pre_ref[k, at[side], :] = pre_ref[k, at[side], :] + (corner(k, side, INNER_LAYER) - past[k, side])
    arrive(t_faces)
    for k in range(2):
        v = v_ref[2, ends[k]] - face("t1", k)
        v_ref[2, ends[k]] = v
        y_ref[2, ends[k]] = m_ref[ends[k]] * v
    for l in order:
        t_ref[2, l] = local_k(lambda n: y_ref[2, n], l)
    mu.append(dot(lambda l: v_ref[2, l], lambda l: y_ref[2, l]))
    for i in range(3):
        dots[i, 2] = dot(lambda l: v_ref[i, l], lambda l: v_ref[2, l])
    arrive(w_edges)
    for side in range(2):
        for l in range(layers):
            d = edge("d", side, l)
            y = (edge("w1", side, l) + edge_part[side, l]) / (d * d + 6.0)
            t_ref[2, l, at[side], :] = t_ref[2, l, at[side], :] - y
    arrive(w_faces)
    for k in range(2):
        d = face("d", k)
        y = (face("w1", k) + pre_ref[k]) / (d * d + 6.0)
        t_ref[2, ends[k]] = t_ref[2, ends[k]] - y
    mu.append(dot(lambda l: t_ref[2, l], lambda l: t_ref[2, l]))
    start_sums(mu, dots, slots, sum_send, sum_recv, me, nx, ny)
    t_edges = edges("t2", t_ref.at[2])
    t_faces = faces("t2", t_ref.at[2])
    for l in order:
        v_ref[3, l] = local_k(lambda n: t_ref[2, n], l)
    arrive(t_edges)
    for l in range(layers):
        for side in range(2):
            v_ref[3, l, at[side], :] = v_ref[3, l, at[side], :] - edge("t2", side, l)
    arrive(t_faces)
    for k in range(2):
        v_ref[3, ends[k]] = v_ref[3, ends[k]] - face("t2", k)

    for copy in sends:
        copy.wait_send()
    all_slots = slots.at[pl.ds(0, count - 1)]
    pltpu.make_async_copy(all_slots, all_slots, sum_send).wait()
    pltpu.make_async_copy(all_slots, all_slots, sum_recv).wait()
    total = jnp.sum(slots[...], axis=0)
    names = [("mu", i) for i in range(2 * ITERS)] + sorted(dots)
    got = {
        name: jnp.broadcast_to(total[:, k : k + 1], total.shape) for k, name in enumerate(names)
    }
    mu = [got["mu", i] for i in range(2 * ITERS)]
    sol, res, norms = coefficients(mu, got, float(cells))
    for k, value in enumerate(norms + sol[:ITERS] + res[1:]):
        coef_ref[k] = value[0, 0]


def start_sums(mu, dots, slots, sum_send, sum_recv, me, nx, ny):
    lane = lax.broadcasted_iota(jnp.int32, (1, slots.shape[-1]), 1)
    line = jnp.zeros(lane.shape, jnp.float32)
    for k, value in enumerate(mu + [dots[name] for name in sorted(dots)]):
        line = jnp.where(lane == k, value, line)
    slots[me] = line

    def send(x, y):
        pltpu.make_async_remote_copy(
            src_ref=slots.at[me],
            dst_ref=slots.at[me],
            send_sem=sum_send,
            recv_sem=sum_recv,
            device_id=(x, y),
            device_id_type=MESH,
        ).start()

    ix, iy = lax.axis_index("gx"), lax.axis_index("gy")
    y_at = [lax.rem(iy + k, ny) for k in range(ny)]

    def send_line(k, carry):
        x = ix + k
        x = jnp.where(x >= nx, x - nx, x)
        for y in y_at[1:] + y_at[:1]:
            send(x, y)
        return carry

    lax.fori_loop(1, nx, send_line, 0)
    for y in y_at[1:]:
        send(ix, y)


def finish(coef, v_ref, y_ref, sol_ref, res_ref, norms_ref):
    for i in range(ITERS):
        norms_ref[i] = coef[i]
    for l in range(v_ref.shape[1]):
        sol = coef[ITERS] * y_ref[0, l]
        res = v_ref[0, l]
        for i in range(1, ITERS):
            sol = sol + coef[ITERS + i] * y_ref[i, l]
        for i in range(1, ITERS + 1):
            res = res + coef[2 * ITERS + i - 1] * v_ref[i, l]
        sol_ref[l] = sol
        res_ref[l] = res


def body(right_side, kappa_sq):
    nx, ny = lax.axis_size("gx"), lax.axis_size("gy")
    shape = right_side.shape
    layers, rows, cols = shape
    cells = nx * layers * ny * rows * cols
    f32 = jnp.float32
    dma = pltpu.SemaphoreType.DMA
    whole = pl.BlockSpec(memory_space=pltpu.VMEM)
    smem = pl.BlockSpec(memory_space=pltpu.SMEM)
    out = pl.pallas_call(
        functools.partial(kernel, nx, ny, cells),
        out_shape=(
            pltpu.VMEM((ITERS + 1,) + shape, f32),
            pltpu.VMEM((ITERS,) + shape, f32),
            pltpu.SMEM((3 * ITERS,), f32),
        ),
        in_specs=[pl.BlockSpec(memory_space=pl.ANY)] * 2,
        out_specs=(whole, whole, smem),
        scratch_shapes=[
            pltpu.VMEM((ITERS,) + shape, f32),
            pltpu.VMEM(shape, f32),
            pltpu.VMEM(shape, f32),
            pltpu.VMEM(shape, f32),
            pltpu.VMEM(shape, f32),
            pltpu.VMEM((2, rows, cols), f32),
            pltpu.VMEM((len(FACES), 2, rows, cols), f32),
            pltpu.VMEM((len(FACES), 2, layers, 1, cols), f32),
            pltpu.VMEM((len(FACES), 2, layers, 1, cols), f32),
            pltpu.VMEM((4, 5, 1, cols), f32),
            pltpu.VMEM((4, 5, 1, cols), f32),
            pltpu.VMEM((nx * ny, 1, 128), f32),
            dma((2, layers)),
            dma((len(FACES), 2)),
            dma((len(FACES), 2)),
            dma((len(FACES), 2)),
            dma((len(FACES), 2)),
            dma((3, 4)),
            dma((3, 4)),
            dma(()),
            dma(()),
        ],
        compiler_params=pltpu.CompilerParams(collective_id=0, has_side_effects=True),
    )(right_side, kappa_sq)
    return pl.pallas_call(
        finish,
        out_shape=(
            jax.ShapeDtypeStruct(shape, f32),
            jax.ShapeDtypeStruct(shape, f32),
            jax.ShapeDtypeStruct((ITERS,), f32),
        ),
        in_specs=[smem, whole, whole],
        out_specs=(whole, whole, smem),
    )(out[2], *(pltpu.with_memory_space_constraint(x, pltpu.VMEM) for x in out[:2]))


def solution(mesh):
    return jax.shard_map(
        body,
        mesh=mesh,
        in_specs=(P("gx", "gy", None), P("gx", "gy", None)),
        out_specs=(P("gx", "gy", None), P("gx", "gy", None), P()),
        check_vma=False,
    )
```

time: 26.7 us -> 24.7 us (0.925)
  Pallas kernels: 25.9 us -> 23.9 us
    pallas_call x1, Pallas kernels: 25 us -> 23 us  [body(): pl.pallas_call(functools.partial(kernel, nx, ny, cells), out_shape=(pltpu...]
where the time goes in v1:
time: 24.7 us; the launch traced here: 24.5 us
  Pallas kernels  23.9 us (97%)
  between operations  0.64 us (3%)
    pallas_call x1, Pallas kernels, body(): pl.pallas_call(functools.partial(kernel, nx, ny, cells), out_shape=(pltpu...  23 us
    pallas_call x1, Pallas kernels, body(): pl.pallas_call(finish, out_shape=(jax.ShapeDtypeStruct(shape, f32), jax.S...  0.89 us

profile of v1, /device:TPU:0, one launch (start us, length us, event | category | flops | bytes accessed | tf_op | source)
XLA Modules:
  0.0 24.5 jit_solution(5833784091826382063)
XLA Ops:
  0.6 23.0 %shard_map.49 = (f32[4,4,64,256]{3,2,1,0:T(8,128)S(1)}, f32[3,4,64,256]{3,2,1,0:T(8,128)S(1)}, f32[9]{0:T(128)S(4)}) custom-call(f32[4,64,256]{2,1,0:T(8,128)} %rhs_hbm.1, f32[4,64,256]{2,1,0:T(8,128)} %kappa_hbm.1), custom_call_target="tpu_custom_call" | custom-call | tf_op jit(solution)/shard_map/pallas_call | solution.py:448
  23.6 0.9 %shard_map.50 = (f32[4,64,256]{2,1,0:T(8,128)}, f32[4,64,256]{2,1,0:T(8,128)}, f32[3]{0:T(128)}) custom-call(f32[9]{0:T(128)S(4)} %get-tuple-element.6.coef, f32[4,4,64,256]{3,2,1,0:T(8,128)S(1)} %get-tuple-element.7.v_ref, f32[3,4,64,256]{3,2,1,0:T(8,128)S(1)} %get-tuple-element.8.y_ref), custom_call_target="tpu_custom_call" | custom-call | tf_op jit(solution)/shard_map/pallas_call | solution.py:482

commit v2 on v1

--- a/solution.py
+++ b/solution.py
@@ -57,19 +57,22 @@
 
 FACES = ("y0", "t0", "d", "y1", "t1", "w1", "t2")
 SLOT = {name: i for i, name in enumerate(FACES)}
-OUTER, INNER_ROW, INNER_LAYER, PARTIAL = 1, 2, 3, 4
+TILE = 8
+OUTER, INNER_ROW, INNER_LAYER, PARTIAL, LAST = 1, 2, 3, 4, 5
 
 
 def kernel(
     nx, ny, cells, rhs_hbm, kappa_hbm, *refs,
 ):
     (
-    v_ref, y_ref, coef_ref, t_ref, f_ref, w_ref, d_ref, m_ref, pre_ref, face_ref, edge_out, edge_in,
+    v_ref, y_ref, coef_ref, t_ref, f_ref, w_ref, d_ref, m_ref, pre_ref, near_m, face_ref, edge_out, edge_in,
     corner_out, corner_in, slots, load_sem, face_send, face_recv, edge_send, edge_recv,
     corner_send, corner_recv, sum_send, sum_recv,
     ) = refs
     layers, rows, cols = rhs_hbm.shape
-    assert layers >= 3 and rows >= 3
+    assert layers >= 3 and rows % TILE == 0 and rows >= 6 * TILE
+    cut_w = rows // (4 * TILE) * TILE
+    cut_t, cut_y, cut = cut_w + TILE, cut_w + 2 * TILE, cut_w + 3 * TILE
     ix, iy = lax.axis_index("gx"), lax.axis_index("gy")
     count = nx * ny
     me = ix * ny + iy
@@ -129,13 +132,21 @@
         down = jnp.where(last, 0.0, pltpu.roll(x, rows - 1, 0))
         return across(x) + (up + down)
 
-    def local_k(get, l):
-        x = get(l)
-        out = d_ref[l] * x - lateral(x)
+    def local_k(ref, l, lo=0, hi=rows):
+        a, b = max(lo - TILE, 0), min(hi + TILE, rows)
+        x = ref[l, a:b]
+        up, down = pltpu.roll(x, 1, 0), pltpu.roll(x, b - a - 1, 0)
+        if a == 0:
+            up = jnp.where(row[: b - a] == 0, 0.0, up)
+        if b == rows:
+            down = jnp.where(row[: b - a] == b - a - 1, 0.0, down)
+        mid = slice(lo - a, hi - a)
+        x = x[mid]
+        out = d_ref[l, lo:hi] * x - (across(x) + (up[mid] + down[mid]))
         if l > 0:
-            out = out - get(l - 1)
+            out = out - ref[l - 1, lo:hi]
         if l < layers - 1:
-            out = out - get(l + 1)
+            out = out - ref[l + 1, lo:hi]
         return out
 
     def tile_sum(x):
@@ -156,46 +167,41 @@
         sends.append(copy)
         return copy
 
-    def edges(name, src):
+    def edges(name, src, side):
+        n = SLOT[name]
+        for l in range(layers):
+            edge_out[n, side, l] = src[l, at[side], :]
+        copy = remote(
+            edge_out.at[n, side], edge_in.at[n, 1 - side],
+            edge_send.at[n, side], edge_recv.at[n, 1 - side], (ix, y_of[side]),
+        )
+        copy.start()
+        return [copy]
+
+    def faces(name, src, part, lo, hi):
         n = SLOT[name]
         out = []
-        for side in range(2):
-            for l in range(layers):
-                edge_out[n, side, l] = src[l, at[side], :]
-        for side in range(2):
+        for k in range(2):
             copy = remote(
-                edge_out.at[n, side], edge_in.at[n, 1 - side],
-                edge_send.at[n, side], edge_recv.at[n, 1 - side], (ix, y_of[side]),
+                src.at[ends[k], pl.ds(lo, hi - lo)], face_ref.at[n, 1 - k, pl.ds(lo, hi - lo)],
+                face_send.at[n, part, k], face_recv.at[n, part, 1 - k], (x_of[k], iy),
             )
             copy.start()
             out.append(copy)
         return out
 
-    def faces(name, src):
-        n = SLOT[name]
+    def corners(n, side, start, size):
         out = []
         for k in range(2):
+            q, there = 2 * k + side, 2 * (1 - k) + 1 - side
             copy = remote(
-                src.at[ends[k]], face_ref.at[n, 1 - k],
-                face_send.at[n, k], face_recv.at[n, 1 - k], (x_of[k], iy),
+                corner_out.at[q, pl.ds(start, size)], corner_in.at[there, pl.ds(start, size)],
+                corner_send.at[n, q], corner_recv.at[n, there], (x_of[k], y_of[side]),
             )
             copy.start()
             out.append(copy)
         return out
 
-    def corners(n, start, size):
-        out = []
-        for k in range(2):
-            for side in range(2):
-                q, there = 2 * k + side, 2 * (1 - k) + 1 - side
-                copy = remote(
-                    corner_out.at[q, pl.ds(start, size)], corner_in.at[there, pl.ds(start, size)],
-                    corner_send.at[n, q], corner_recv.at[n, there], (x_of[k], y_of[side]),
-                )
-                copy.start()
-                out.append(copy)
-        return out
-
     def arrive(copies):
         for copy in copies:
             copy.wait_recv()
@@ -211,34 +217,47 @@
 
     mu, dots = ([], {})
 
-    def full_t(j):
+    def full_t(j, lo, hi):
         for l in range(layers):
-            t = t_ref[j, l]
+            t = t_ref[j, l, lo:hi]
             for k in range(2):
                 if l == ends[k]:
-                    t = t - face(f"y{j}", k)
-            f_ref[l] = t
+                    t = t - face_ref[SLOT[f"y{j}"], k, lo:hi]
+            f_ref[l, lo:hi] = t
             for side in range(2):
-                f_ref[l, at[side], :] = f_ref[l, at[side], :] - edge(f"y{j}", side, l)
-        mu.append(dot(lambda l: f_ref[l], lambda l: f_ref[l]))
-
-    def next_v(j):
+                if (0, rows)[side] in (lo, hi):
+                    f_ref[l, at[side], :] = f_ref[l, at[side], :] - edge(f"y{j}", side, l)
+
+    def next_v(j, lo, hi):
         for l in order:
-            v = local_k(lambda n: f_ref[n], l)
+            v = local_k(f_ref, l, lo, hi)
             if l in ends:
-                v = v + y_ref[j, l]
-            v_ref[j + 1, l] = v
+                v = v + y_ref[j, l, lo:hi]
+            v_ref[j + 1, l, lo:hi] = v
             for side in range(2):
-                v_ref[j + 1, l, at[side], :] = v_ref[j + 1, l, at[side], :] + y_ref[j, l, at[side], :]
-
-    def next_rows(j, part):
+                if (0, rows)[side] in (lo, hi):
+                    line = y_ref[j, l, at[side], :]
+                    v_ref[j + 1, l, at[side], :] = v_ref[j + 1, l, at[side], :] + line
+
+    def next_rows(j, part, sides):
         for l in order:
-            for side in range(2):
+            for side in sides:
                 line = v_ref[j + 1, l, at[side], :] - edge(f"t{j}", side, l)
                 for k in range(2):
                     if l == ends[k]:
                         line = line + 2.0 * corner(k, side, part)
                 v_ref[j + 1, l, at[side], :] = line
+
+    def next_y(j, which, lo, hi):
+        for l in which:
+            y_ref[j, l, lo:hi] = m_ref[l, lo:hi] * v_ref[j, l, lo:hi]
+
+    def next_ends(j, lo, hi):
+        for k in range(2):
+            l = ends[k]
+            v = v_ref[j + 1, l, lo:hi] - face_ref[SLOT[f"t{j}"], k, lo:hi]
+            v_ref[j + 1, l, lo:hi] = v
+            y_ref[j + 1, l, lo:hi] = m_ref[l, lo:hi] * v
 
     for l in order:
         for copy in loads[l]:
@@ -248,63 +267,77 @@
         m_ref[l] = 1.0 / (d * d + 6.0)
         y_ref[0, l] = m_ref[l] * v_ref[0, l]
     pl.semaphore_wait(barrier, greetings)
-    y_edges = edges("y0", y_ref.at[0])
-    for k in range(2):
-        for side in range(2):
-            corner_out[2 * k + side, 0] = y_ref[0, ends[k], at[side], :]
-    y_corners = corners(0, 0, 1)
-    y_faces = faces("y0", y_ref.at[0])
+    y, t = y_ref.at[0], t_ref.at[0]
+    got = {}
+    for side in range(2):
+        got["ye", 1 - side] = edges("y0", y, side)
+        for k in range(2):
+            corner_out[2 * k + side, 0] = y[ends[k], at[side], :]
+        got["yc", 1 - side] = corners(0, side, 0, 1)
+    got["y", 0] = faces("y0", y, 0, 0, cut)
     for l in order:
-        t_ref[0, l] = local_k(lambda n: y_ref[0, n], l)
-    t_edges = edges("t0", t_ref.at[0])
-    t_faces = faces("t0", t_ref.at[0])
-    d_edges = edges("d", d_ref)
-    d_faces = faces("d", d_ref)
+        t[l] = local_k(y, l)
+    got["t", 0] = faces("t0", t, 0, 0, cut)
+    for side in range(2):
+        got["te", 1 - side] = edges("t0", t, side)
+    got["y", 1] = faces("y0", y, 1, cut, rows)
+    got["t", 1] = faces("t0", t, 1, cut, rows)
     mu.append(dot(lambda l: v_ref[0, l], lambda l: y_ref[0, l]))
     dots[0, 0] = dot(lambda l: v_ref[0, l], lambda l: v_ref[0, l])
-    arrive(y_edges + y_faces)
-    full_t(0)
-    next_v(0)
-    arrive(t_edges + y_corners)
-    next_rows(0, 0)
-    for l in inside:
-        y_ref[1, l] = m_ref[l] * v_ref[1, l]
-    arrive(t_faces)
-    for k in range(2):
-        v = v_ref[1, ends[k]] - face("t0", k)
-        v_ref[1, ends[k]] = v
-        y_ref[1, ends[k]] = m_ref[ends[k]] * v
-    y_edges = edges("y1", y_ref.at[1])
-    for k in range(2):
-        for side in range(2):
+    y, t = y_ref.at[1], t_ref.at[1]
+    y_edges, y_corners, y_faces = [], [], []
+    t_edges, t_corners, t_faces = [], [], []
+    w_edges, w_faces = [], []
+    spans = [
+        [(0, cut), (0, cut_y), (0, cut_t), (0, cut_w)],
+        [(cut, rows), (cut_y, rows), (cut_t, rows), (cut_w, rows)],
+    ]
+    for part in range(2):
+        side, (span, span_y, span_t, span_w) = part, spans[part]
+        arrive(got["ye", side])
+        if part == 0:
+            d_edges = edges("d", d_ref, 0) + edges("d", d_ref, 1)
+            d_faces = faces("d", d_ref, 0, 0, rows)
+        arrive(got["y", part])
+        full_t(0, *span)
+        next_v(0, *span_y)
+        arrive(got["te", side] + got["yc", side])
+        next_rows(0, 0, (side,))
+        next_y(1, inside, *span_y)
+        arrive(got["t", part])
+        next_ends(0, *span_y)
+        y_faces += faces("y1", y, part, *span_y)
+        y_edges += edges("y1", y, side)
+        for k in range(2):
             q = 2 * k + side
-            corner_out[q, OUTER] = y_ref[1, ends[k], at[side], :]
-            corner_out[q, INNER_ROW] = y_ref[1, ends[k], at_second[side], :]
-            corner_out[q, INNER_LAYER] = y_ref[1, seconds[k], at[side], :]
-    y_corners = corners(1, OUTER, 3)
-    y_faces = faces("y1", y_ref.at[1])
-    for l in order:
-        t_ref[1, l] = local_k(lambda n: y_ref[1, n], l)
-    t_edges = edges("t1", t_ref.at[1])
-    for k in range(2):
-        for side in range(2):
-            corner_out[2 * k + side, PARTIAL] = t_ref[1, ends[k], at[side], :]
-    t_corners = corners(2, PARTIAL, 1)
-    t_faces = faces("t1", t_ref.at[1])
-    for l in order:
-        w_ref[l] = local_k(lambda n: t_ref[1, n], l)
-    w_edges = edges("w1", w_ref)
-    w_faces = faces("w1", w_ref)
+            corner_out[q, OUTER] = y[ends[k], at[side], :]
+            corner_out[q, INNER_ROW] = y[ends[k], at_second[side], :]
+            corner_out[q, INNER_LAYER] = y[seconds[k], at[side], :]
+        y_corners += corners(1, side, OUTER, 3)
+        lo, hi = span_t
+        for l in order:
+            t[l, lo:hi] = local_k(y, l, lo, hi)
+        t_faces += faces("t1", t, part, lo, hi)
+        t_edges += edges("t1", t, side)
+        for k in range(2):
+            corner_out[2 * k + side, PARTIAL] = t[ends[k], at[side], :]
+        t_corners += corners(2, side, PARTIAL, 1)
+        lo, hi = span_w
+        for l in order:
+            w_ref[l, lo:hi] = local_k(t, l, lo, hi)
+        w_faces += faces("w1", w_ref, part, lo, hi)
+        w_edges += edges("w1", w_ref, side)
+    mu.append(dot(lambda l: f_ref[l], lambda l: f_ref[l]))
     mu.append(dot(lambda l: v_ref[1, l], lambda l: y_ref[1, l]))
     for i in range(2):
         dots[i, 1] = dot(lambda l: v_ref[i, l], lambda l: v_ref[1, l])
     arrive(y_edges + y_faces)
-    full_t(1)
-    next_v(1)
+    full_t(1, 0, rows)
+    next_v(1, 0, rows)
+    mu.append(dot(lambda l: f_ref[l], lambda l: f_ref[l]))
     arrive(t_edges + y_corners + t_corners + d_edges)
-    next_rows(1, OUTER)
-    for l in inside:
-        y_ref[2, l] = m_ref[l] * v_ref[2, l]
+    next_rows(1, OUTER, range(2))
+    next_y(2, inside, 0, rows)
     past = {
         (k, side): corner(k, side, PARTIAL) - (edge("y1", side, ends[k]) + face_ref[SLOT["y1"], k, at[side], :])
         for k in range(2)
@@ -336,16 +369,25 @@
         for side in range(2):
             pre_ref[k, at[side], :] = pre_ref[k, at[side], :] + corner(k, side, OUTER)
         a = pre_ref[k]
-        pre_ref[k] = lateral(a) - face("d", k) * a - f_ref[ends[k]]
+        d = face("d", k)
+        near_m[k] = 1.0 / (d * d + 6.0)
+        pre_ref[k] = lateral(a) - d * a - f_ref[ends[k]]
         for side in range(2):
             pre_ref[k, at[side], :] = pre_ref[k, at[side], :] + (corner(k, side, INNER_LAYER) - past[k, side])
     arrive(t_faces)
-    for k in range(2):
-        v = v_ref[2, ends[k]] - face("t1", k)
-        v_ref[2, ends[k]] = v
-        y_ref[2, ends[k]] = m_ref[ends[k]] * v
+    next_ends(1, 0, rows)
+    y, t = y_ref.at[2], t_ref.at[2]
+    y_corners, t_edges = [], []
+    for side in range(2):
+        for k in range(2):
+            corner_out[2 * k + side, LAST] = y[ends[k], at[side], :]
+        y_corners += corners(3, side, LAST, 1)
     for l in order:
-        t_ref[2, l] = local_k(lambda n: y_ref[2, n], l)
+        t[l] = local_k(y, l)
+        f_ref[l] = t[l]
+    for side in range(2):
+        t_edges += edges("t2", t, side)
+    t_faces = faces("t2", t, 0, 0, rows)
     mu.append(dot(lambda l: v_ref[2, l], lambda l: y_ref[2, l]))
     for i in range(3):
         dots[i, 2] = dot(lambda l: v_ref[i, l], lambda l: v_ref[2, l])
@@ -354,22 +396,21 @@
         for l in range(layers):
             d = edge("d", side, l)
             y = (edge("w1", side, l) + edge_part[side, l]) / (d * d + 6.0)
-            t_ref[2, l, at[side], :] = t_ref[2, l, at[side], :] - y
+            f_ref[l, at[side], :] = f_ref[l, at[side], :] - y
+    part = sum(f_ref[l] * f_ref[l] for l in inside)
+    line = sums_line(mu, dots, slots.shape[-1])
     arrive(w_faces)
     for k in range(2):
-        d = face("d", k)
-        y = (face("w1", k) + pre_ref[k]) / (d * d + 6.0)
-        t_ref[2, ends[k]] = t_ref[2, ends[k]] - y
-    mu.append(dot(lambda l: t_ref[2, l], lambda l: t_ref[2, l]))
-    start_sums(mu, dots, slots, sum_send, sum_recv, me, nx, ny)
-    t_edges = edges("t2", t_ref.at[2])
-    t_faces = faces("t2", t_ref.at[2])
-    for l in order:
-        v_ref[3, l] = local_k(lambda n: t_ref[2, n], l)
-    arrive(t_edges)
-    for l in range(layers):
-        for side in range(2):
-            v_ref[3, l, at[side], :] = v_ref[3, l, at[side], :] - edge("t2", side, l)
+        t = f_ref[ends[k]] - near_m[k] * (face("w1", k) + pre_ref[k])
+        f_ref[ends[k]] = t
+        part = part + t * t
+    mu.append(tile_sum(part))
+    lane = lax.broadcasted_iota(jnp.int32, line.shape, 1)
+    slots[me] = jnp.where(lane == place(("mu", 2 * ITERS - 1)), mu[-1], line)
+    start_sums(slots, sum_send, sum_recv, me, nx, ny)
+    next_v(2, 0, rows)
+    arrive(t_edges + y_corners)
+    next_rows(2, LAST, range(2))
     arrive(t_faces)
     for k in range(2):
         v_ref[3, ends[k]] = v_ref[3, ends[k]] - face("t2", k)
@@ -380,23 +421,34 @@
     pltpu.make_async_copy(all_slots, all_slots, sum_send).wait()
     pltpu.make_async_copy(all_slots, all_slots, sum_recv).wait()
     total = jnp.sum(slots[...], axis=0)
-    names = [("mu", i) for i in range(2 * ITERS)] + sorted(dots)
-    got = {
-        name: jnp.broadcast_to(total[:, k : k + 1], total.shape) for k, name in enumerate(names)
-    }
-    mu = [got["mu", i] for i in range(2 * ITERS)]
+
+    def whole(name):
+        n = place(name)
+        return jnp.broadcast_to(total[:, n : n + 1], total.shape)
+
+    mu = [whole(("mu", i)) for i in range(2 * ITERS)]
+    got = {name: whole(name) for name in dots}
     sol, res, norms = coefficients(mu, got, float(cells))
     for k, value in enumerate(norms + sol[:ITERS] + res[1:]):
         coef_ref[k] = value[0, 0]
 
 
-def start_sums(mu, dots, slots, sum_send, sum_recv, me, nx, ny):
-    lane = lax.broadcasted_iota(jnp.int32, (1, slots.shape[-1]), 1)
+def place(name):
+    names = [("mu", i) for i in range(2 * ITERS)]
+    names += [(i, j) for j in range(ITERS) for i in range(j + 1)]
+    return names.index(name)
+
+
+def sums_line(mu, dots, size):
+    lane = lax.broadcasted_iota(jnp.int32, (1, size), 1)
     line = jnp.zeros(lane.shape, jnp.float32)
-    for k, value in enumerate(mu + [dots[name] for name in sorted(dots)]):
-        line = jnp.where(lane == k, value, line)
-    slots[me] = line
-
+    named = [(("mu", i), value) for i, value in enumerate(mu)] + list(dots.items())
+    for name, value in named:
+        line = jnp.where(lane == place(name), value, line)
+    return line
+
+
+def start_sums(slots, sum_send, sum_recv, me, nx, ny):
     def send(x, y):
         pltpu.make_async_remote_copy(
             src_ref=slots.at[me],
@@ -461,19 +513,20 @@
             pltpu.VMEM(shape, f32),
             pltpu.VMEM(shape, f32),
             pltpu.VMEM((2, rows, cols), f32),
+            pltpu.VMEM((2, rows, cols), f32),
             pltpu.VMEM((len(FACES), 2, rows, cols), f32),
             pltpu.VMEM((len(FACES), 2, layers, 1, cols), f32),
             pltpu.VMEM((len(FACES), 2, layers, 1, cols), f32),
-            pltpu.VMEM((4, 5, 1, cols), f32),
-            pltpu.VMEM((4, 5, 1, cols), f32),
+            pltpu.VMEM((4, 6, 1, cols), f32),
+            pltpu.VMEM((4, 6, 1, cols), f32),
             pltpu.VMEM((nx * ny, 1, 128), f32),
             dma((2, layers)),
+            dma((len(FACES), 2, 2)),
+            dma((len(FACES), 2, 2)),
             dma((len(FACES), 2)),
             dma((len(FACES), 2)),
-            dma((len(FACES), 2)),
-            dma((len(FACES), 2)),
-            dma((3, 4)),
-            dma((3, 4)),
+            dma((4, 4)),
+            dma((4, 4)),
             dma(()),
             dma(()),
         ],

time: 24.7 us -> 23.7 us (0.960)
  Pallas kernels: 23.9 us -> 22.8 us
    pallas_call x1, Pallas kernels: 23 us -> 22 us  [body(): pl.pallas_call(functools.partial(kernel, nx, ny, cells), out_shape=(pltpu...]
where the time goes in v2:
time: 23.7 us; the launch traced here: 23.5 us
  Pallas kernels  22.8 us (96%)
  between operations  0.64 us (3%)
    pallas_call x1, Pallas kernels, body(): pl.pallas_call(functools.partial(kernel, nx, ny, cells), out_shape=(pltpu...  22 us
    pallas_call x1, Pallas kernels, body(): pl.pallas_call(finish, out_shape=(jax.ShapeDtypeStruct(shape, f32), jax.S...  0.89 us

profile of v2, /device:TPU:0, one launch (start us, length us, event | category | flops | bytes accessed | tf_op | source)
XLA Modules:
  0.0 23.5 jit_solution(4176831609962125640)
XLA Ops:
  0.6 22.0 %shard_map.49 = (f32[4,4,64,256]{3,2,1,0:T(8,128)S(1)}, f32[3,4,64,256]{3,2,1,0:T(8,128)S(1)}, f32[9]{0:T(128)S(4)}) custom-call(f32[4,64,256]{2,1,0:T(8,128)} %rhs_hbm.1, f32[4,64,256]{2,1,0:T(8,128)} %kappa_hbm.1), custom_call_target="tpu_custom_call" | custom-call | tf_op jit(solution)/shard_map/pallas_call | solution.py:500
  22.6 0.9 %shard_map.50 = (f32[4,64,256]{2,1,0:T(8,128)}, f32[4,64,256]{2,1,0:T(8,128)}, f32[3]{0:T(128)}) custom-call(f32[9]{0:T(128)S(4)} %get-tuple-element.6.coef, f32[4,4,64,256]{3,2,1,0:T(8,128)S(1)} %get-tuple-element.7.v_ref, f32[3,4,64,256]{3,2,1,0:T(8,128)S(1)} %get-tuple-element.8.y_ref), custom_call_target="tpu_custom_call" | custom-call | tf_op jit(solution)/shard_map/pallas_call | solution.py:535

commit v3 on v2

--- a/solution.py
+++ b/solution.py
@@ -57,6 +57,11 @@
 
 FACES = ("y0", "t0", "d", "y1", "t1", "w1", "t2")
 SLOT = {name: i for i, name in enumerate(FACES)}
+SAME = {"t2": "y0"}
+SPLIT = ("y0", "t0")
+ARRIVALS = tuple((name, part) for name in SPLIT for part in range(2)) + tuple(
+    (name, 0) for name in ("d", "y1", "t1", "w1")
+)
 TILE = 8
 OUTER, INNER_ROW, INNER_LAYER, PARTIAL, LAST = 1, 2, 3, 4, 5
 
@@ -79,14 +84,10 @@
     ends, seconds = (0, layers - 1), (1, layers - 2)
     order = [0, layers - 1] + list(range(1, layers - 1))
     inside = list(range(1, layers - 1))
-    loads = {}
-    for l in order:
-        loads[l] = (
-            pltpu.make_async_copy(kappa_hbm.at[l], d_ref.at[l], load_sem.at[0, l]),
-            pltpu.make_async_copy(rhs_hbm.at[l], v_ref.at[0, l], load_sem.at[1, l]),
-        )
-        for copy in loads[l]:
-            copy.start()
+    load_k = pltpu.make_async_copy(kappa_hbm, d_ref, load_sem.at[0])
+    load_r = pltpu.make_async_copy(rhs_hbm, v_ref.at[0], load_sem.at[1])
+    load_k.start()
+    load_r.start()
 
     barrier = pltpu.get_barrier_semaphore()
     x_of = (lax.rem(ix + nx - 1, nx), lax.rem(ix + 1, nx))
@@ -157,54 +158,54 @@
 
     at = [pl.ds((0, rows - 1)[side], 1) for side in range(2)]
     at_second = [pl.ds((1, rows - 2)[side], 1) for side in range(2)]
-    sends = []
-
     def remote(src, dst, send, recv, device):
-        copy = pltpu.make_async_remote_copy(
+        pltpu.make_async_remote_copy(
             src_ref=src, dst_ref=dst, send_sem=send, recv_sem=recv,
             device_id=device, device_id_type=MESH,
-        )
-        sends.append(copy)
-        return copy
+        ).start()
+
+    def wait(ref, sem):
+        pltpu.make_async_copy(ref, ref, sem).wait()
+
+    def edge_sem(name, side):
+        return edge_recv.at[ARRIVALS.index((name, side if name in SPLIT else 0))]
 
     def edges(name, src, side):
         n = SLOT[name]
         for l in range(layers):
             edge_out[n, side, l] = src[l, at[side], :]
-        copy = remote(
-            edge_out.at[n, side], edge_in.at[n, 1 - side],
-            edge_send.at[n, side], edge_recv.at[n, 1 - side], (ix, y_of[side]),
-        )
-        copy.start()
-        return [copy]
+        sem = edge_sem(SAME.get(name, name), 1 - side)
+        remote(edge_out.at[n, side], edge_in.at[n, 1 - side], edge_send, sem, (ix, y_of[side]))
+
+    def wait_edges(name, side=None):
+        if side is None:
+            wait(edge_in.at[SLOT[name]], edge_sem(name, 0))
+        else:
+            wait(edge_in.at[SLOT[name], side], edge_sem(SAME.get(name, name), side))
+
+    def face_sem(name, part):
+        return face_recv.at[ARRIVALS.index((name, part if name in SPLIT else 0))]
 
     def faces(name, src, part, lo, hi):
-        n = SLOT[name]
-        out = []
-        for k in range(2):
-            copy = remote(
-                src.at[ends[k], pl.ds(lo, hi - lo)], face_ref.at[n, 1 - k, pl.ds(lo, hi - lo)],
-                face_send.at[n, part, k], face_recv.at[n, part, 1 - k], (x_of[k], iy),
+        n, span = SLOT[name], pl.ds(lo, hi - lo)
+        sem = face_sem(SAME.get(name, name), part)
+        for k in range(2):
+            remote(
+                src.at[ends[k], span], face_ref.at[n, 1 - k, span], face_send, sem, (x_of[k], iy)
             )
-            copy.start()
-            out.append(copy)
-        return out
-
-    def corners(n, side, start, size):
-        out = []
-        for k in range(2):
-            q, there = 2 * k + side, 2 * (1 - k) + 1 - side
-            copy = remote(
-                corner_out.at[q, pl.ds(start, size)], corner_in.at[there, pl.ds(start, size)],
-                corner_send.at[n, q], corner_recv.at[n, there], (x_of[k], y_of[side]),
+
+    def wait_faces(name, part=0, lo=0, hi=rows):
+        sem = face_sem(SAME.get(name, name), part)
+        wait(face_ref.at[SLOT[name], :, pl.ds(lo, hi - lo)], sem)
+
+    def corners(side, start, size, again=True):
+        sem = corner_recv.at[1 - side if again else 2]
+        for k in range(2):
+            span = pl.ds(start, size)
+            remote(
+                corner_out.at[side, k, span], corner_in.at[1 - side, 1 - k, span],
+                corner_send, sem, (x_of[k], y_of[side]),
             )
-            copy.start()
-            out.append(copy)
-        return out
-
-    def arrive(copies):
-        for copy in copies:
-            copy.wait_recv()
 
     def edge(name, side, l):
         return edge_in[SLOT[name], side, l]
@@ -213,7 +214,7 @@
         return face_ref[SLOT[name], k]
 
     def corner(k, side, part):
-        return corner_in[2 * k + side, part]
+        return corner_in[side, k, part]
 
     mu, dots = ([], {})
 
@@ -259,83 +260,84 @@
             v_ref[j + 1, l, lo:hi] = v
             y_ref[j + 1, l, lo:hi] = m_ref[l, lo:hi] * v
 
+    load_k.wait()
     for l in order:
-        for copy in loads[l]:
-            copy.wait()
         d = 6.0 + d_ref[l]
         d_ref[l] = d
         m_ref[l] = 1.0 / (d * d + 6.0)
+    load_r.wait()
+    for l in order:
         y_ref[0, l] = m_ref[l] * v_ref[0, l]
     pl.semaphore_wait(barrier, greetings)
     y, t = y_ref.at[0], t_ref.at[0]
-    got = {}
-    for side in range(2):
-        got["ye", 1 - side] = edges("y0", y, side)
-        for k in range(2):
-            corner_out[2 * k + side, 0] = y[ends[k], at[side], :]
-        got["yc", 1 - side] = corners(0, side, 0, 1)
-    got["y", 0] = faces("y0", y, 0, 0, cut)
+    for side in range(2):
+        edges("y0", y, side)
+        for k in range(2):
+            corner_out[side, k, 0] = y[ends[k], at[side], :]
+        corners(side, 0, 1)
+    faces("y0", y, 0, 0, cut)
     for l in order:
         t[l] = local_k(y, l)
-    got["t", 0] = faces("t0", t, 0, 0, cut)
-    for side in range(2):
-        got["te", 1 - side] = edges("t0", t, side)
-    got["y", 1] = faces("y0", y, 1, cut, rows)
-    got["t", 1] = faces("t0", t, 1, cut, rows)
+    faces("t0", t, 0, 0, cut)
+    for side in range(2):
+        edges("t0", t, side)
+    faces("y0", y, 1, cut, rows)
+    faces("t0", t, 1, cut, rows)
     mu.append(dot(lambda l: v_ref[0, l], lambda l: y_ref[0, l]))
     dots[0, 0] = dot(lambda l: v_ref[0, l], lambda l: v_ref[0, l])
     y, t = y_ref.at[1], t_ref.at[1]
-    y_edges, y_corners, y_faces = [], [], []
-    t_edges, t_corners, t_faces = [], [], []
-    w_edges, w_faces = [], []
     spans = [
         [(0, cut), (0, cut_y), (0, cut_t), (0, cut_w)],
         [(cut, rows), (cut_y, rows), (cut_t, rows), (cut_w, rows)],
     ]
     for part in range(2):
         side, (span, span_y, span_t, span_w) = part, spans[part]
-        arrive(got["ye", side])
+        wait_edges("y0", side)
         if part == 0:
-            d_edges = edges("d", d_ref, 0) + edges("d", d_ref, 1)
-            d_faces = faces("d", d_ref, 0, 0, rows)
-        arrive(got["y", part])
+            edges("d", d_ref, 0)
+            edges("d", d_ref, 1)
+            faces("d", d_ref, 0, 0, rows)
+        wait_faces("y0", part, *span)
         full_t(0, *span)
         next_v(0, *span_y)
-        arrive(got["te", side] + got["yc", side])
+        wait_edges("t0", side)
+        wait(corner_in.at[side, :, 0], corner_recv.at[side])
         next_rows(0, 0, (side,))
         next_y(1, inside, *span_y)
-        arrive(got["t", part])
+        wait_faces("t0", part, *span)
         next_ends(0, *span_y)
-        y_faces += faces("y1", y, part, *span_y)
-        y_edges += edges("y1", y, side)
-        for k in range(2):
-            q = 2 * k + side
-            corner_out[q, OUTER] = y[ends[k], at[side], :]
-            corner_out[q, INNER_ROW] = y[ends[k], at_second[side], :]
-            corner_out[q, INNER_LAYER] = y[seconds[k], at[side], :]
-        y_corners += corners(1, side, OUTER, 3)
+        faces("y1", y, part, *span_y)
+        edges("y1", y, side)
+        for k in range(2):
+            corner_out[side, k, OUTER] = y[ends[k], at[side], :]
+            corner_out[side, k, INNER_ROW] = y[ends[k], at_second[side], :]
+            corner_out[side, k, INNER_LAYER] = y[seconds[k], at[side], :]
+        corners(side, OUTER, 3, False)
         lo, hi = span_t
         for l in order:
             t[l, lo:hi] = local_k(y, l, lo, hi)
-        t_faces += faces("t1", t, part, lo, hi)
-        t_edges += edges("t1", t, side)
-        for k in range(2):
-            corner_out[2 * k + side, PARTIAL] = t[ends[k], at[side], :]
-        t_corners += corners(2, side, PARTIAL, 1)
+        faces("t1", t, part, lo, hi)
+        edges("t1", t, side)
+        for k in range(2):
+            corner_out[side, k, PARTIAL] = t[ends[k], at[side], :]
+        corners(side, PARTIAL, 1, False)
         lo, hi = span_w
         for l in order:
             w_ref[l, lo:hi] = local_k(t, l, lo, hi)
-        w_faces += faces("w1", w_ref, part, lo, hi)
-        w_edges += edges("w1", w_ref, side)
+        faces("w1", w_ref, part, lo, hi)
+        edges("w1", w_ref, side)
     mu.append(dot(lambda l: f_ref[l], lambda l: f_ref[l]))
     mu.append(dot(lambda l: v_ref[1, l], lambda l: y_ref[1, l]))
     for i in range(2):
         dots[i, 1] = dot(lambda l: v_ref[i, l], lambda l: v_ref[1, l])
-    arrive(y_edges + y_faces)
+    wait_edges("y1")
+    wait_faces("y1")
     full_t(1, 0, rows)
     next_v(1, 0, rows)
     mu.append(dot(lambda l: f_ref[l], lambda l: f_ref[l]))
-    arrive(t_edges + y_corners + t_corners + d_edges)
+    wait_edges("t1")
+    wait_edges("d")
+    wait(corner_in.at[:, :, pl.ds(OUTER, 4)], corner_recv.at[2])
     next_rows(1, OUTER, range(2))
     next_y(2, inside, 0, rows)
     past = {
@@ -363,7 +365,7 @@
                 if l == ends[k]:
                     part = part + (corner(k, side, INNER_ROW) - past[k, side])
             edge_part[side, l] = part
-    arrive(d_faces)
+    wait_faces("d")
     for k in range(2):
         pre_ref[k] = y_ref[1, ends[k]]
         for side in range(2):
@@ -374,24 +376,23 @@
         pre_ref[k] = lateral(a) - d * a - f_ref[ends[k]]
         for side in range(2):
             pre_ref[k, at[side], :] = pre_ref[k, at[side], :] + (corner(k, side, INNER_LAYER) - past[k, side])
-    arrive(t_faces)
+    wait_faces("t1")
     next_ends(1, 0, rows)
     y, t = y_ref.at[2], t_ref.at[2]
-    y_corners, t_edges = [], []
-    for side in range(2):
-        for k in range(2):
-            corner_out[2 * k + side, LAST] = y[ends[k], at[side], :]
-        y_corners += corners(3, side, LAST, 1)
+    for side in range(2):
+        for k in range(2):
+            corner_out[side, k, LAST] = y[ends[k], at[side], :]
+        corners(side, LAST, 1)
     for l in order:
         t[l] = local_k(y, l)
         f_ref[l] = t[l]
     for side in range(2):
-        t_edges += edges("t2", t, side)
-    t_faces = faces("t2", t, 0, 0, rows)
+        edges("t2", t, side)
+    faces("t2", t, 0, 0, rows)
     mu.append(dot(lambda l: v_ref[2, l], lambda l: y_ref[2, l]))
     for i in range(3):
         dots[i, 2] = dot(lambda l: v_ref[i, l], lambda l: v_ref[2, l])
-    arrive(w_edges)
+    wait_edges("w1")
     for side in range(2):
         for l in range(layers):
             d = edge("d", side, l)
@@ -399,7 +400,7 @@
             f_ref[l, at[side], :] = f_ref[l, at[side], :] - y
     part = sum(f_ref[l] * f_ref[l] for l in inside)
     line = sums_line(mu, dots, slots.shape[-1])
-    arrive(w_faces)
+    wait_faces("w1")
     for k in range(2):
         t = f_ref[ends[k]] - near_m[k] * (face("w1", k) + pre_ref[k])
         f_ref[ends[k]] = t
@@ -409,14 +410,17 @@
     slots[me] = jnp.where(lane == place(("mu", 2 * ITERS - 1)), mu[-1], line)
     start_sums(slots, sum_send, sum_recv, me, nx, ny)
     next_v(2, 0, rows)
-    arrive(t_edges + y_corners)
+    for side in range(2):
+        wait_edges("t2", side)
+        wait(corner_in.at[side, :, LAST], corner_recv.at[side])
     next_rows(2, LAST, range(2))
-    arrive(t_faces)
+    wait_faces("t2")
     for k in range(2):
         v_ref[3, ends[k]] = v_ref[3, ends[k]] - face("t2", k)
 
-    for copy in sends:
-        copy.wait_send()
+    wait(face_ref, face_send)
+    wait(edge_in, edge_send)
+    wait(corner_in, corner_send)
     all_slots = slots.at[pl.ds(0, count - 1)]
     pltpu.make_async_copy(all_slots, all_slots, sum_send).wait()
     pltpu.make_async_copy(all_slots, all_slots, sum_recv).wait()
@@ -517,16 +521,16 @@
             pltpu.VMEM((len(FACES), 2, rows, cols), f32),
             pltpu.VMEM((len(FACES), 2, layers, 1, cols), f32),
             pltpu.VMEM((len(FACES), 2, layers, 1, cols), f32),
-            pltpu.VMEM((4, 6, 1, cols), f32),
-            pltpu.VMEM((4, 6, 1, cols), f32),
+            pltpu.VMEM((2, 2, 6, 1, cols), f32),
+            pltpu.VMEM((2, 2, 6, 1, cols), f32),
             pltpu.VMEM((nx * ny, 1, 128), f32),
-            dma((2, layers)),
-            dma((len(FACES), 2, 2)),
-            dma((len(FACES), 2, 2)),
-            dma((len(FACES), 2)),
-            dma((len(FACES), 2)),
-            dma((4, 4)),
-            dma((4, 4)),
+            dma((2,)),
+            dma(()),
+            dma((len(ARRIVALS),)),
+            dma(()),
+            dma((len(ARRIVALS),)),
+            dma(()),
+            dma((3,)),
             dma(()),
             dma(()),
         ],

time: 23.7 us -> 22.7 us (0.958)
  Pallas kernels: 22.8 us -> 21.9 us
    pallas_call x1, Pallas kernels: 22 us -> 21.1 us  [body(): pl.pallas_call(functools.partial(kernel, nx, ny, cells), out_shape=(pltpu...]
where the time goes in v3:
time: 22.7 us; the launch traced here: 22.6 us
  Pallas kernels  21.9 us (96%)
  between operations  0.64 us (3%)
    pallas_call x1, Pallas kernels, body(): pl.pallas_call(functools.partial(kernel, nx, ny, cells), out_shape=(pltpu...  21.1 us
    pallas_call x1, Pallas kernels, body(): pl.pallas_call(finish, out_shape=(jax.ShapeDtypeStruct(shape, f32), jax.S...  0.89 us

profile of v3, /device:TPU:0, one launch (start us, length us, event | category | flops | bytes accessed | tf_op | source)
XLA Modules:
  0.0 22.6 jit_solution(7025900702906887710)
XLA Ops:
  0.6 21.1 %shard_map.49 = (f32[4,4,64,256]{3,2,1,0:T(8,128)S(1)}, f32[3,4,64,256]{3,2,1,0:T(8,128)S(1)}, f32[9]{0:T(128)S(4)}) custom-call(f32[4,64,256]{2,1,0:T(8,128)} %rhs_hbm.1, f32[4,64,256]{2,1,0:T(8,128)} %kappa_hbm.1), custom_call_target="tpu_custom_call" | custom-call | tf_op jit(solution)/shard_map/pallas_call | solution.py:504
  21.7 0.9 %shard_map.50 = (f32[4,64,256]{2,1,0:T(8,128)}, f32[4,64,256]{2,1,0:T(8,128)}, f32[3]{0:T(128)}) custom-call(f32[9]{0:T(128)S(4)} %get-tuple-element.6.coef, f32[4,4,64,256]{3,2,1,0:T(8,128)S(1)} %get-tuple-element.7.v_ref, f32[3,4,64,256]{3,2,1,0:T(8,128)S(1)} %get-tuple-element.8.y_ref), custom_call_target="tpu_custom_call" | custom-call | tf_op jit(solution)/shard_map/pallas_call | solution.py:539

commit v4 on v3

--- a/solution.py
+++ b/solution.py
@@ -55,12 +55,12 @@
     return sol, res, norms
 
 
-FACES = ("y0", "t0", "d", "y1", "t1", "w1", "t2")
+FACES = ("y0", "t0", "y1", "d", "t1", "w1", "t2")
 SLOT = {name: i for i, name in enumerate(FACES)}
 SAME = {"t2": "y0"}
 SPLIT = ("y0", "t0")
 ARRIVALS = tuple((name, part) for name in SPLIT for part in range(2)) + tuple(
-    (name, 0) for name in ("d", "y1", "t1", "w1")
+    (name, 0) for name in ("y1", "t1", "w1", "d")
 )
 TILE = 8
 OUTER, INNER_ROW, INNER_LAYER, PARTIAL, LAST = 1, 2, 3, 4, 5
@@ -71,8 +71,8 @@
 ):
     (
     v_ref, y_ref, coef_ref, t_ref, f_ref, w_ref, d_ref, m_ref, pre_ref, near_m, face_ref, edge_out, edge_in,
-    corner_out, corner_in, slots, load_sem, face_send, face_recv, edge_send, edge_recv,
-    corner_send, corner_recv, sum_send, sum_recv,
+    corner_out, corner_in, slots, load_sem, face_recv, edge_send, edge_recv,
+    corner_recv, sum_send, sum_recv,
     ) = refs
     layers, rows, cols = rhs_hbm.shape
     assert layers >= 3 and rows % TILE == 0 and rows >= 6 * TILE
@@ -84,6 +84,7 @@
     ends, seconds = (0, layers - 1), (1, layers - 2)
     order = [0, layers - 1] + list(range(1, layers - 1))
     inside = list(range(1, layers - 1))
+    face_send, corner_send = load_sem.at[0], load_sem.at[1]
     load_k = pltpu.make_async_copy(kappa_hbm, d_ref, load_sem.at[0])
     load_r = pltpu.make_async_copy(rhs_hbm, v_ref.at[0], load_sem.at[1])
     load_k.start()
@@ -113,10 +114,12 @@
 
     if near:
         for x in x_of:
-            for y in y_of:
+            greet(x, iy)
+        for y in y_of:
+            for x in x_of:
                 greet(x, y)
         lax.fori_loop(1, ny, greet_y, 0)
-        lax.fori_loop(1, nx, greet_x, 0)
+        lax.fori_loop(2, nx - 1, greet_x, 0)
         greetings = nx - 1 + ny - 1 + 4
     else:
         lax.fori_loop(1, count, greet_any, 0)
@@ -170,11 +173,15 @@
     def edge_sem(name, side):
         return edge_recv.at[ARRIVALS.index((name, side if name in SPLIT else 0))]
 
+    def stage(name, src, side):
+        for l in range(layers):
+            edge_out[SLOT[name], side, l] = src[l, at[side], :]
+
     def edges(name, src, side):
         n = SLOT[name]
-        for l in range(layers):
-            edge_out[n, side, l] = src[l, at[side], :]
-        sem = edge_sem(SAME.get(name, name), 1 - side)
+        if name != "y0":
+            stage(name, src, side)
+        sem = edge_sem("t1" if name == "d" else SAME.get(name, name), 1 - side)
         remote(edge_out.at[n, side], edge_in.at[n, 1 - side], edge_send, sem, (ix, y_of[side]))
 
     def wait_edges(name, side=None):
@@ -268,12 +275,14 @@
     load_r.wait()
     for l in order:
         y_ref[0, l] = m_ref[l] * v_ref[0, l]
+    y, t = y_ref.at[0], t_ref.at[0]
+    for side in range(2):
+        stage("y0", y, side)
+        for k in range(2):
+            corner_out[side, k, 0] = y[ends[k], at[side], :]
     pl.semaphore_wait(barrier, greetings)
-    y, t = y_ref.at[0], t_ref.at[0]
     for side in range(2):
         edges("y0", y, side)
-        for k in range(2):
-            corner_out[side, k, 0] = y[ends[k], at[side], :]
         corners(side, 0, 1)
     faces("y0", y, 0, 0, cut)
     for l in order:
@@ -335,8 +344,7 @@
     full_t(1, 0, rows)
     next_v(1, 0, rows)
     mu.append(dot(lambda l: f_ref[l], lambda l: f_ref[l]))
-    wait_edges("t1")
-    wait_edges("d")
+    wait(edge_in.at[pl.ds(SLOT["d"], 2)], edge_sem("t1", 0))
     wait(corner_in.at[:, :, pl.ds(OUTER, 4)], corner_recv.at[2])
     next_rows(1, OUTER, range(2))
     next_y(2, inside, 0, rows)
@@ -434,7 +442,7 @@
     got = {name: whole(name) for name in dots}
     sol, res, norms = coefficients(mu, got, float(cells))
     for k, value in enumerate(norms + sol[:ITERS] + res[1:]):
-        coef_ref[k] = value[0, 0]
+        coef_ref[k] = value
 
 
 def place(name):
@@ -464,32 +472,35 @@
         ).start()
 
     ix, iy = lax.axis_index("gx"), lax.axis_index("gy")
-    y_at = [lax.rem(iy + k, ny) for k in range(ny)]
+    for k in range(ny - 1):
+        send(ix, jnp.where(iy <= k, k + 1, k))
 
     def send_line(k, carry):
-        x = ix + k
-        x = jnp.where(x >= nx, x - nx, x)
-        for y in y_at[1:] + y_at[:1]:
+        x = jnp.where(ix <= k, k + 1, k)
+        for y in range(ny):
             send(x, y)
         return carry
 
-    lax.fori_loop(1, nx, send_line, 0)
-    for y in y_at[1:]:
-        send(ix, y)
+    lax.fori_loop(0, nx - 1, send_line, 0, unroll=nx * ny <= 64)
 
 
 def finish(coef, v_ref, y_ref, sol_ref, res_ref, norms_ref):
-    for i in range(ITERS):
-        norms_ref[i] = coef[i]
+    cols = v_ref.shape[-1]
+    lines = [jnp.concatenate([coef[k]] * (cols // coef.shape[-1]), axis=1) for k in range(3 * ITERS)]
     for l in range(v_ref.shape[1]):
-        sol = coef[ITERS] * y_ref[0, l]
+        sol = lines[ITERS] * y_ref[0, l]
         res = v_ref[0, l]
         for i in range(1, ITERS):
-            sol = sol + coef[ITERS + i] * y_ref[i, l]
+            sol = sol + lines[ITERS + i] * y_ref[i, l]
         for i in range(1, ITERS + 1):
-            res = res + coef[2 * ITERS + i - 1] * v_ref[i, l]
+            res = res + lines[2 * ITERS + i - 1] * v_ref[i, l]
         sol_ref[l] = sol
         res_ref[l] = res
+    lane = lax.broadcasted_iota(jnp.int32, coef.shape[1:], 1)
+    line = coef[0]
+    for i in range(1, ITERS):
+        line = jnp.where(lane == i, coef[i], line)
+    norms_ref[...] = line[0, :ITERS]
 
 
 def body(right_side, kappa_sq):
@@ -500,16 +511,15 @@
     f32 = jnp.float32
     dma = pltpu.SemaphoreType.DMA
     whole = pl.BlockSpec(memory_space=pltpu.VMEM)
-    smem = pl.BlockSpec(memory_space=pltpu.SMEM)
     out = pl.pallas_call(
         functools.partial(kernel, nx, ny, cells),
         out_shape=(
             pltpu.VMEM((ITERS + 1,) + shape, f32),
             pltpu.VMEM((ITERS,) + shape, f32),
-            pltpu.SMEM((3 * ITERS,), f32),
+            pltpu.VMEM((3 * ITERS, 1, 128), f32),
         ),
         in_specs=[pl.BlockSpec(memory_space=pl.ANY)] * 2,
-        out_specs=(whole, whole, smem),
+        out_specs=(whole, whole, whole),
         scratch_shapes=[
             pltpu.VMEM((ITERS,) + shape, f32),
             pltpu.VMEM(shape, f32),
@@ -525,11 +535,9 @@
             pltpu.VMEM((2, 2, 6, 1, cols), f32),
             pltpu.VMEM((nx * ny, 1, 128), f32),
             dma((2,)),
-            dma(()),
             dma((len(ARRIVALS),)),
             dma(()),
-            dma((len(ARRIVALS),)),
-            dma(()),
+            dma((len(ARRIVALS) - 1,)),
             dma((3,)),
             dma(()),
             dma(()),
@@ -543,9 +551,9 @@
             jax.ShapeDtypeStruct(shape, f32),
             jax.ShapeDtypeStruct((ITERS,), f32),
         ),
-        in_specs=[smem, whole, whole],
-        out_specs=(whole, whole, smem),
-    )(out[2], *(pltpu.with_memory_space_constraint(x, pltpu.VMEM) for x in out[:2]))
+        in_specs=[whole, whole, whole],
+        out_specs=(whole, whole, whole),
+    )(*(pltpu.with_memory_space_constraint(x, pltpu.VMEM) for x in (out[2], out[0], out[1])))
 
 
 def solution(mesh):

time: 22.7 us -> 22.6 us (level)
  no operation moved by 1% of the time
where the time goes in v4:
time: 22.6 us; the launch traced here: 22.4 us
  Pallas kernels  21.8 us (96%)
  between operations  0.64 us (3%)
    pallas_call x1, Pallas kernels, body(): pl.pallas_call(functools.partial(kernel, nx, ny, cells), out_shape=(pltpu...  20.9 us
    pallas_call x1, Pallas kernels, body(): pl.pallas_call(finish, out_shape=(jax.ShapeDtypeStruct(shape, f32), jax.S...  0.87 us

profile of v4, /device:TPU:0, one launch (start us, length us, event | category | flops | bytes accessed | tf_op | source)
XLA Modules:
  0.0 22.4 jit_solution(1224218944310928930)
XLA Ops:
  0.6 20.9 %shard_map.49 = (f32[4,4,64,256]{3,2,1,0:T(8,128)S(1)}, f32[3,4,64,256]{3,2,1,0:T(8,128)S(1)}, f32[9,1,128]{2,1,0:T(1,128)S(1)}) custom-call(f32[4,64,256]{2,1,0:T(8,128)} %rhs_hbm.1, f32[4,64,256]{2,1,0:T(8,128)} %kappa_hbm.1), custom_call_target="tpu_custom_call" | custom-call | tf_op jit(solution)/shard_map/pallas_call | solution.py:514
  21.5 0.9 %shard_map.50 = (f32[4,64,256]{2,1,0:T(8,128)}, f32[4,64,256]{2,1,0:T(8,128)}, f32[3]{0:T(128)}) custom-call(f32[9,1,128]{2,1,0:T(1,128)S(1)} %get-tuple-element.6.coef, f32[4,4,64,256]{3,2,1,0:T(8,128)S(1)} %get-tuple-element.7.v_ref, f32[3,4,64,256]{3,2,1,0:T(8,128)S(1)} %get-tuple-element.8.y_ref), custom_call_target="tpu_custom_call" | custom-call | tf_op jit(solution)/shard_map/pallas_call | solution.py:547

commit v5 on v4

--- a/solution.py
+++ b/solution.py
@@ -171,7 +171,8 @@
         pltpu.make_async_copy(ref, ref, sem).wait()
 
     def edge_sem(name, side):
-        return edge_recv.at[ARRIVALS.index((name, side if name in SPLIT else 0))]
+        first = name in SPLIT
+        return edge_recv.at[side if first else ARRIVALS.index((name, 0)) - 2]
 
     def stage(name, src, side):
         for l in range(layers):
@@ -179,7 +180,7 @@
 
     def edges(name, src, side):
         n = SLOT[name]
-        if name != "y0":
+        if name not in SPLIT + ("d",):
             stage(name, src, side)
         sem = edge_sem("t1" if name == "d" else SAME.get(name, name), 1 - side)
         remote(edge_out.at[n, side], edge_in.at[n, 1 - side], edge_send, sem, (ix, y_of[side]))
@@ -278,20 +279,26 @@
     y, t = y_ref.at[0], t_ref.at[0]
     for side in range(2):
         stage("y0", y, side)
+        stage("d", d_ref, side)
         for k in range(2):
             corner_out[side, k, 0] = y[ends[k], at[side], :]
+    for l in order:
+        t[l] = local_k(y, l)
+    for side in range(2):
+        stage("t0", t, side)
     pl.semaphore_wait(barrier, greetings)
     for side in range(2):
-        edges("y0", y, side)
         corners(side, 0, 1)
     faces("y0", y, 0, 0, cut)
-    for l in order:
-        t[l] = local_k(y, l)
+    for side in range(2):
+        edges("y0", y, side)
     faces("t0", t, 0, 0, cut)
     for side in range(2):
         edges("t0", t, side)
     faces("y0", y, 1, cut, rows)
     faces("t0", t, 1, cut, rows)
+    for side in range(2):
+        edges("d", d_ref, side)
     mu.append(dot(lambda l: v_ref[0, l], lambda l: y_ref[0, l]))
     dots[0, 0] = dot(lambda l: v_ref[0, l], lambda l: v_ref[0, l])
     y, t = y_ref.at[1], t_ref.at[1]
@@ -301,15 +308,12 @@
     ]
     for part in range(2):
         side, (span, span_y, span_t, span_w) = part, spans[part]
-        wait_edges("y0", side)
+        wait(edge_in.at[pl.ds(SLOT["y0"], 2), side], edge_sem("y0", side))
         if part == 0:
-            edges("d", d_ref, 0)
-            edges("d", d_ref, 1)
             faces("d", d_ref, 0, 0, rows)
         wait_faces("y0", part, *span)
         full_t(0, *span)
         next_v(0, *span_y)
-        wait_edges("t0", side)
         wait(corner_in.at[side, :, 0], corner_recv.at[side])
         next_rows(0, 0, (side,))
         next_y(1, inside, *span_y)
@@ -411,12 +415,13 @@
     wait_faces("w1")
     for k in range(2):
         t = f_ref[ends[k]] - near_m[k] * (face("w1", k) + pre_ref[k])
-        f_ref[ends[k]] = t
         part = part + t * t
     mu.append(tile_sum(part))
     lane = lax.broadcasted_iota(jnp.int32, line.shape, 1)
     slots[me] = jnp.where(lane == place(("mu", 2 * ITERS - 1)), mu[-1], line)
     start_sums(slots, sum_send, sum_recv, me, nx, ny)
+    for k in range(2):
+        f_ref[ends[k]] = f_ref[ends[k]] - near_m[k] * (face("w1", k) + pre_ref[k])
     next_v(2, 0, rows)
     for side in range(2):
         wait_edges("t2", side)
@@ -487,15 +492,17 @@
 def finish(coef, v_ref, y_ref, sol_ref, res_ref, norms_ref):
     cols = v_ref.shape[-1]
     lines = [jnp.concatenate([coef[k]] * (cols // coef.shape[-1]), axis=1) for k in range(3 * ITERS)]
-    for l in range(v_ref.shape[1]):
+    half = v_ref.shape[1] // pl.num_programs(0)
+    for n in range(half):
+        l = pl.program_id(0) * half + n
         sol = lines[ITERS] * y_ref[0, l]
         res = v_ref[0, l]
         for i in range(1, ITERS):
             sol = sol + lines[ITERS + i] * y_ref[i, l]
         for i in range(1, ITERS + 1):
             res = res + lines[2 * ITERS + i - 1] * v_ref[i, l]
-        sol_ref[l] = sol
-        res_ref[l] = res
+        sol_ref[n] = sol
+        res_ref[n] = res
     lane = lax.broadcasted_iota(jnp.int32, coef.shape[1:], 1)
     line = coef[0]
     for i in range(1, ITERS):
@@ -537,7 +544,7 @@
             dma((2,)),
             dma((len(ARRIVALS),)),
             dma(()),
-            dma((len(ARRIVALS) - 1,)),
+            dma((len(ARRIVALS) - 3,)),
             dma((3,)),
             dma(()),
             dma(()),
@@ -551,8 +558,9 @@
             jax.ShapeDtypeStruct(shape, f32),
             jax.ShapeDtypeStruct((ITERS,), f32),
         ),
+        grid=(2,),
         in_specs=[whole, whole, whole],
-        out_specs=(whole, whole, whole),
+        out_specs=(pl.BlockSpec((layers // 2, rows, cols), lambda h: (h, 0, 0)),) * 2 + (whole,),
     )(*(pltpu.with_memory_space_constraint(x, pltpu.VMEM) for x in (out[2], out[0], out[1])))
 
 

time: 22.6 us -> 22.5 us (level)
  no operation moved by 1% of the time
where the time goes in v5:
time: 22.5 us; the launch traced here: 22.4 us
  Pallas kernels  21.7 us (96%)
  between operations  0.64 us (3%)
    pallas_call x1, Pallas kernels, body(): pl.pallas_call(functools.partial(kernel, nx, ny, cells), out_shape=(pltpu...  20.9 us
    pallas_call x1, Pallas kernels, body(): pl.pallas_call(finish, out_shape=(jax.ShapeDtypeStruct(shape, f32), jax.S...  0.86 us

profile of v5, /device:TPU:0, one launch (start us, length us, event | category | flops | bytes accessed | tf_op | source)
XLA Modules:
  0.0 22.4 jit_solution(8812569172910069148)
XLA Ops:
  0.6 20.9 %shard_map.49 = (f32[4,4,64,256]{3,2,1,0:T(8,128)S(1)}, f32[3,4,64,256]{3,2,1,0:T(8,128)S(1)}, f32[9,1,128]{2,1,0:T(1,128)S(1)}) custom-call(f32[4,64,256]{2,1,0:T(8,128)} %rhs_hbm.1, f32[4,64,256]{2,1,0:T(8,128)} %kappa_hbm.1), custom_call_target="tpu_custom_call" | custom-call | tf_op jit(solution)/shard_map/pallas_call | solution.py:521
  21.5 0.9 %shard_map.50 = (f32[4,64,256]{2,1,0:T(8,128)}, f32[4,64,256]{2,1,0:T(8,128)}, f32[3]{0:T(128)}) custom-call(f32[9,1,128]{2,1,0:T(1,128)S(1)} %get-tuple-element.6.coef, f32[4,4,64,256]{3,2,1,0:T(8,128)S(1)} %get-tuple-element.7.v_ref, f32[3,4,64,256]{3,2,1,0:T(8,128)S(1)} %get-tuple-element.8.y_ref), custom_call_target="tpu_custom_call" | custom-call | tf_op jit(solution)/shard_map/pallas_call | solution.py:554

commit v6 on v5

--- a/solution.py
+++ b/solution.py
@@ -87,8 +87,6 @@
     face_send, corner_send = load_sem.at[0], load_sem.at[1]
     load_k = pltpu.make_async_copy(kappa_hbm, d_ref, load_sem.at[0])
     load_r = pltpu.make_async_copy(rhs_hbm, v_ref.at[0], load_sem.at[1])
-    load_k.start()
-    load_r.start()
 
     barrier = pltpu.get_barrier_semaphore()
     x_of = (lax.rem(ix + nx - 1, nx), lax.rem(ix + 1, nx))
@@ -115,6 +113,8 @@
     if near:
         for x in x_of:
             greet(x, iy)
+        load_k.start()
+        load_r.start()
         for y in y_of:
             for x in x_of:
                 greet(x, y)
@@ -122,6 +122,8 @@
         lax.fori_loop(2, nx - 1, greet_x, 0)
         greetings = nx - 1 + ny - 1 + 4
     else:
+        load_k.start()
+        load_r.start()
         lax.fori_loop(1, count, greet_any, 0)
         greetings = count - 1
 

time: 22.5 us -> 22.5 us (level)
  no operation moved by 1% of the time
where the time goes in v6:
time: 22.5 us; the launch traced here: 22.4 us
  Pallas kernels  21.7 us (96%)
  between operations  0.64 us (3%)
    pallas_call x1, Pallas kernels, body(): pl.pallas_call(functools.partial(kernel, nx, ny, cells), out_shape=(pltpu...  20.9 us
    pallas_call x1, Pallas kernels, body(): pl.pallas_call(finish, out_shape=(jax.ShapeDtypeStruct(shape, f32), jax.S...  0.86 us

profile of v6, /device:TPU:0, one launch (start us, length us, event | category | flops | bytes accessed | tf_op | source)
XLA Modules:
  0.0 22.4 jit_solution(1358505479831768407)
XLA Ops:
  0.6 20.9 %shard_map.49 = (f32[4,4,64,256]{3,2,1,0:T(8,128)S(1)}, f32[3,4,64,256]{3,2,1,0:T(8,128)S(1)}, f32[9,1,128]{2,1,0:T(1,128)S(1)}) custom-call(f32[4,64,256]{2,1,0:T(8,128)} %rhs_hbm.1, f32[4,64,256]{2,1,0:T(8,128)} %kappa_hbm.1), custom_call_target="tpu_custom_call" | custom-call | tf_op jit(solution)/shard_map/pallas_call | solution.py:523
  21.5 0.9 %shard_map.50 = (f32[4,64,256]{2,1,0:T(8,128)}, f32[4,64,256]{2,1,0:T(8,128)}, f32[3]{0:T(128)}) custom-call(f32[9,1,128]{2,1,0:T(1,128)S(1)} %get-tuple-element.6.coef, f32[4,4,64,256]{3,2,1,0:T(8,128)S(1)} %get-tuple-element.7.v_ref, f32[3,4,64,256]{3,2,1,0:T(8,128)S(1)} %get-tuple-element.8.y_ref), custom_call_target="tpu_custom_call" | custom-call | tf_op jit(solution)/shard_map/pallas_call | solution.py:556
